TPU v7x, 32 devices: a whole 2x2x4 slice. The times are simulated.
32 devices in a mesh: pts: 8 (over y, x, core), cand: 4 (over z).
Axes of the slice: x: 2, y: 2, z: 4, core: 2. Of those that a mesh axis runs over, the one named last changes fastest.
Arguments:
- points: bfloat16 [8192, 1024], P('pts'), may hold values from -6 to 6
- weights: float32 [8192], P('pts'), may hold values from 0.5 to 5
- coverage: float32 [8192], P('pts'), may hold values from -0.5 to 1
- candidates: bfloat16 [4096, 1024], P('cand'), may hold values from -6 to 6
- picks: int32 [64], replicated, may hold values from 0 to 4095
Outputs:
- gains: float32 [4096], P('cand')
- top_gains: float32 [64], replicated
- new_coverage: float32 [8192], P('pts')
All inputs are finite; a program needn't handle non-finite values.
Results may differ from a plain program's by a relative error of at most 0.0003.
Values may be sent and summed in bfloat16 or wider, within the bound.
A program may use at most 64 MiB of HBM per device.

v0:
```python
import jax
import jax.numpy as jnp
from jax import lax
from jax.sharding import PartitionSpec as P

TOPK = 64


def joined(x, axis, combine):
    everything = lax.all_gather(x, axis)
    leading = everything[0]

    def hop(k, so_far):
        return combine(so_far, everything[k])

    return lax.fori_loop(1, lax.axis_size(axis), hop, leading)


def best_values(first, second):
    return lax.top_k(jnp.concatenate([first, second]), TOPK)[0]


def on_device(points, weights, coverage, candidates, picks):
    scale = points.shape[1] ** (-0.5)
    total = points.shape[0] * lax.axis_size("pts")
    cand_rows = candidates.shape[0]
    offset = lax.axis_index("cand") * cand_rows
    sims = jnp.dot(points, candidates.T, preferred_element_type=jnp.float32) * scale
    partial_value = (
        jnp.sum(weights[:, None] * jnp.maximum(sims - coverage[:, None], 0.0), axis=0) / total
    )
    gains = lax.psum(partial_value, "pts")
    top_gains = joined(lax.top_k(gains, TOPK)[0], "cand", best_values)
    columns = offset + jnp.arange(cand_rows, dtype=jnp.int32)
    chosen = jnp.any(picks[:, None] == columns[None, :], axis=0)
    local_best = jnp.max(jnp.where(chosen[None, :], sims, -1e30), axis=1)
    best_sim = lax.pmax(local_best, "cand")
    new_coverage = jnp.maximum(coverage, best_sim)
    return (gains, top_gains, new_coverage)


def solution(mesh):
    placed = (P("pts", None), P("pts"), P("pts"), P("cand", None), P())
    return jax.shard_map(
        on_device, mesh=mesh, in_specs=placed, out_specs=(P("cand"), P(), P("pts")), check_vma=False
    )
```

profile of v0, /device:TPU:0, one launch (start us, length us, event | category | flops | bytes accessed | tf_op | source)
XLA Modules:
  0.0 56.5 jit_solution(17969848759909569890)
XLA Ops:
  0.6 0.0 copy-start
  0.7 0.9 %compare_reduce_fusion = pred[1024]{0:T(1024)(128)(4,1)S(1)} fusion(s32[1024]{0:T(1024)S(1)} %iota_add_fusion, s32[64]{0:T(128)} %param.11), kind=kLoop, calls=%fused_computation.4 | loop fusion | flops 130048 | bytes 5376 | tf_op jit(solution)/shard_map/reduce_or | solution.py:35
  1.6 0.7 %copy-done = bf16[1024,1024]{1,0:T(8,128)(2,1)S(1)} copy-done((bf16[1024,1024]{1,0:T(8,128)(2,1)S(1)}, bf16[1024,1024]{1,0:T(8,128)(2,1)}, u32[]{:S(2)}) %copy-start) | copy-done | bytes 2097176
  2.2 0.0 copy-start.3
  2.2 4.4 %select_reduce_fusion = (f32[1024]{0:T(1024)S(1)}, f32[1024]{0:T(1024)S(1)}) fusion(pred[1024]{0:T(1024)(128)(4,1)S(1)} %compare_reduce_fusion, f32[1024]{0:T(1024)} %param.9, f32[1024]{0:T(1024)} %param.8, bf16[1024,1024]{1,0:T(8,128)(2,1)S(1)} %copy-done, bf16[1024,1024]{1,0:T(8,128)(2,1)} %param.10), kind=kOutput, calls=%fused_computation.2 | convolution fusion | flops 2154821632 | bytes 4211712 | tf_op jit(solution)/shard_map/dot_general | solution.py:28
  6.6 15.2 %psum.7 = f32[1024]{0:T(1024)S(1)} all-reduce(f32[1024]{0:T(1024)S(1)} %broadcast_multiply_fusion), channel_id=1, replica_groups=mesh['pts'=8,'cand'=4] {'pts'}, use_global_device_ids=true, to_apply=%region_1.0 | all-reduce | flops 1024 | bytes 8192 | tf_op jit(solution)/shard_map/psum | solution.py:32
  21.8 4.4 %top_k.14 = (f32[1024]{0:T(1024)S(1)}, s32[1024]{0:T(1024)}) sort(f32[1024]{0:T(1024)S(1)} %psum.7, s32[1024]{0:T(1024)S(1)} %iota.11), dimensions={0}, to_apply=%region_2.0 | sort | flops 10240 | bytes 16384 | tf_op jit(solution)/shard_map/top_k | solution.py:33
  26.2 0.0 copy-done.3
  26.2 0.6 %dynamic-slice = u32[1]{0:T(128)} dynamic-slice(u32[32]{0:T(128)S(1)} %copy-done.3, u32[]{:T(128)S(6)} %add.47), dynamic_slice_sizes={1} | dynamic-slice | bytes 12
  27.5 0.1 slice_dynamic-update-slice_fusion
  27.6 11.9 %all-reduce = f32[256]{0:T(256)S(1)} all-reduce(f32[256]{0:T(256)S(1)} %slice_dynamic-update-slice_fusion), channel_id=2, replica_groups=mesh['pts'=8,'cand'=4] {'cand'}, use_global_device_ids=true, to_apply=%add | all-reduce | flops 256 | bytes 2048
  39.5 0.1 reshape.14
  39.6 8.0 %while.15 = (s32[]{:T(128)}, f32[64]{0:T(128)S(1)}, f32[4,64]{1,0:T(4,128)S(1)}, s32[]{:T(128)}, s32[]{:T(128)}, /*index=5*/s32[]{:T(128)}) while((s32[]{:T(128)}, f32[64]{0:T(128)S(1)}, f32[4,64]{1,0:T(4,128)S(1)}, s32[]{:T(128)}, s32[]{:T(128)}, /*index=5*/s32[]{:T(128)}) %tuple.41), condition=%wide.region_5.6_spmd, body=%wide.region_3.5_spmd.sunk | while | flops 1029 | bytes 4211 | solution.py:16
  39.6 0.1 pad_maximum_fusion.2
  39.7 2.6 %top_k.22 = (f32[128]{0:T(128)S(1)}, s32[128]{0:T(128)}) sort(f32[128]{0:T(128)S(1)} %pad_maximum_fusion.2, s32[128]{0:T(128)S(1)} %iota.15), dimensions={0}, to_apply=%region_4.4 | sort | flops 896 | bytes 2048 | tf_op jit(solution)/shard_map/while/body/eval_jaxpr/top_k | solution.py:20
  42.2 0.1 pad_maximum_fusion.2
  42.3 2.6 %top_k.22 = (f32[128]{0:T(128)S(1)}, s32[128]{0:T(128)}) sort(f32[128]{0:T(128)S(1)} %pad_maximum_fusion.2, s32[128]{0:T(128)S(1)} %iota.15), dimensions={0}, to_apply=%region_4.4 | sort | flops 896 | bytes 2048 | tf_op jit(solution)/shard_map/while/body/eval_jaxpr/top_k | solution.py:20
  44.9 0.1 pad_maximum_fusion.2
  45.0 2.6 %top_k.22 = (f32[128]{0:T(128)S(1)}, s32[128]{0:T(128)}) sort(f32[128]{0:T(128)S(1)} %pad_maximum_fusion.2, s32[128]{0:T(128)S(1)} %iota.15), dimensions={0}, to_apply=%region_4.4 | sort | flops 896 | bytes 2048 | tf_op jit(solution)/shard_map/while/body/eval_jaxpr/top_k | solution.py:20
  47.5 8.3 %pmax.7 = f32[1024]{0:T(1024)S(1)} all-reduce(f32[1024]{0:T(1024)S(1)} %get-tuple-element.97), channel_id=1, replica_groups=mesh['pts'=8,'cand'=4] {'cand'}, use_global_device_ids=true, to_apply=%region_8.9 | all-reduce | flops 1024 | bytes 8192 | tf_op jit(solution)/shard_map/pmax | solution.py:37
  55.9 0.0 copy-done.2
  55.9 0.6 %max.13 = f32[1024]{0:T(1024)} maximum(f32[1024]{0:T(1024)S(1)} %copy-done.2, f32[1024]{0:T(1024)S(1)} %pmax.7) | non-fusion elementwise | flops 1024 | bytes 12288 | tf_op jit(solution)/shard_map/max | solution.py:38
  56.5 0.0 copy-done.1
  56.5 0.0 copy-done.4
  (14 shorter events, 0.0 us)
Async XLA Ops:
  0.6 1.6 %copy-start = (bf16[1024,1024]{1,0:T(8,128)(2,1)S(1)}, bf16[1024,1024]{1,0:T(8,128)(2,1)}, u32[]{:S(2)}) copy-start(bf16[1024,1024]{1,0:T(8,128)(2,1)} %param.7) | copy-start | bytes 6291460
  2.2 24.0 %copy-start.3 = (u32[32]{0:T(128)S(1)}, u32[32]{0:T(128)}, u32[]{:S(2)}) copy-start(u32[32]{0:T(128)} %constant.74) | copy-start | bytes 388
  2.2 53.6 %copy-start.2 = (f32[1024]{0:T(1024)S(1)}, f32[1024]{0:T(1024)}, u32[]{:S(2)}) copy-start(f32[1024]{0:T(1024)} %param.9) | copy-start | bytes 12292
  21.8 34.7 %copy-start.1 = (f32[1024]{0:T(1024)}, f32[1024]{0:T(1024)S(1)}, u32[]{:S(2)}) copy-start(f32[1024]{0:T(1024)S(1)} %psum.7) | copy-start | bytes 12292
  47.5 8.9 %copy-start.4 = (f32[64]{0:T(128)}, f32[64]{0:T(128)S(1)}, u32[]{:S(2)}) copy-start(f32[64]{0:T(128)S(1)} %get-tuple-element.93) | copy-start | bytes 772
where the time goes:
time: 56.7 us; the launch traced here: 56.5 us
  blocking collectives  35.4 us (62%)
  other arithmetic  13.9 us (25%)
  matrix products  4.37 us (8%)
  local copies, waits for them, and re-layouts  1.48 us (3%)
  between operations  1.34 us (2%)
    psum x1, blocking collectives, on_device(): gains = lax.psum(partial_value, 'pts')  15.2 us
    unnamed x1, blocking collectives  11.9 us
    pmax x1, blocking collectives, on_device(): best_sim = lax.pmax(local_best, 'cand')  8.34 us
    top_k x3, other arithmetic, best_values(): return lax.top_k(jnp.concatenate([first, second]), TOPK)[0]  7.7 us
    top_k x1, other arithmetic, on_device(): top_gains = joined(lax.top_k(gains, TOPK)[0], 'cand', best_values)  4.43 us
    dot_general x1, matrix products, on_device(): jnp.dot(points, candidates.T, preferred_element_type=jnp.float32) * scale  4.37 us
    unnamed x13, local copies, waits for them, and re-layouts  1.37 us

commit v1 on v0

v1 whole, which is shorter than its diff:
```python
import functools

import jax
import jax.numpy as jnp
from jax import lax
from jax.experimental import pallas as pl
from jax.experimental.pallas import tpu as pltpu
from jax.sharding import PartitionSpec as P

TOPK = 64
LANES = 128
MESH = pl.DeviceIdType.MESH
F32 = jnp.float32
LOW = -1e30
HIGH = 3e38
CHUNK = 256


def column_tile(row):
    return jnp.transpose(jnp.broadcast_to(row, (LANES, LANES)))


def ranked(columns, rows, count):
    wide = [jnp.broadcast_to(row, (8, LANES)) for row in rows]
    above = [jnp.zeros((8, LANES), F32) for _ in rows]
    for column in columns:
        for g in range(column.shape[0] // 8):
            value = column[g * 8 : (g + 1) * 8, :]
            above = [a + jnp.where(value > w, 1.0, 0.0) for a, w in zip(above, wide)]
    place = lax.broadcasted_iota(jnp.int32, (count, LANES), 0).astype(F32)
    best = jnp.full((count, LANES), HIGH, F32)
    for a, row in zip(above, rows):
        total = jnp.sum(a, axis=0, keepdims=True)
        best = jnp.minimum(best, jnp.where(total <= place, row, HIGH))
    return jnp.min(best, axis=1, keepdims=True)


def as_row(column):
    count = column.shape[0]
    wide = jnp.broadcast_to(column, (count, LANES))
    if count < LANES:
        wide = jnp.concatenate([wide, jnp.full((LANES - count, LANES), -1.0, F32)], axis=0)
    return jnp.transpose(wide)[0:1, :]


def kernel(
    n_pts, n_cand, points, weights, coverage, candidates, picks, gains_out, top_out, cover_out,
    p_buf, c_buf, w_buf, v_buf, k_buf, w_col, v_col, g_acc, b_acc, part, parts, best, bests,
    top, tops, g_col, gains_buf, top_buf, cover_buf,
    in_sem, small_sem, out_sem, part_send, part_recv, best_send, best_recv, top_send, top_recv,
):
    rows, depth = points.shape
    cands = candidates.shape[0]
    me, mz = lax.axis_index("pts"), lax.axis_index("cand")
    n_p, n_c = rows // CHUNK, cands // CHUNK
    tiles_p, tiles_c = rows // LANES, cands // LANES
    scale = depth ** (-0.5)

    small = [
        pltpu.make_async_copy(weights, w_buf, small_sem.at[0]),
        pltpu.make_async_copy(coverage, v_buf, small_sem.at[1]),
        pltpu.make_async_copy(picks, k_buf, small_sem.at[2]),
    ]
    for copy in small:
        copy.start()
    loads = {}
    order = []
    for i in range(max(n_p, n_c)):
        if i < n_c:
            order.append(("c", i))
        if i < n_p:
            order.append(("p", i))
    for at, (kind, i) in enumerate(order):
        src, dst = (points, p_buf) if kind == "p" else (candidates, c_buf)
        span = pl.ds(i * CHUNK, CHUNK)
        loads[kind, i] = pltpu.make_async_copy(src.at[span, :], dst.at[span, :], in_sem.at[at])
        loads[kind, i].start()

    barrier = pltpu.get_barrier_semaphore()
    for k in range(1, n_pts):
        pl.semaphore_signal(
            barrier, inc=1, device_id={"pts": lax.rem(me + k, n_pts)}, device_id_type=MESH
        )
    for k in range(1, n_cand):
        pl.semaphore_signal(
            barrier, inc=1, device_id={"cand": lax.rem(mz + k, n_cand)}, device_id_type=MESH
        )

    for copy in small:
        copy.wait()
    column = mz * cands + lax.broadcasted_iota(jnp.int32, (tiles_c, LANES), 0) * LANES
    column = column + lax.broadcasted_iota(jnp.int32, (tiles_c, LANES), 1)
    chosen = jnp.zeros((tiles_c, LANES), jnp.bool_)
    for k in range(picks.shape[0]):
        chosen = chosen | (column == k_buf[k])
    penalty = jnp.where(chosen, 0.0, LOW)
    w_row = w_buf[...] * (scale / (rows * n_pts))
    v_row = v_buf[...] * (1.0 / scale)
    for t in range(tiles_p):
        w_col[t * LANES : (t + 1) * LANES, :] = column_tile(w_row[t : t + 1, :])
        v_col[t * LANES : (t + 1) * LANES, :] = column_tile(v_row[t : t + 1, :])

    def block(pi, ci):
        ps = pl.ds(pi * CHUNK, CHUNK)
        sims = lax.dot_general(
            p_buf[ps, :], c_buf[pl.ds(ci * CHUNK, CHUNK), :],
            (((1,), (1,)), ((), ())), preferred_element_type=F32,
        )
        w, v = w_col[ps, :], v_col[ps, :]
        found = None
        for l in range(CHUNK // LANES):
            tile = ci * (CHUNK // LANES) + l
            x = sims[:, l * LANES : (l + 1) * LANES]
            value = jnp.maximum(x - v, 0.0) * w
            value = jnp.sum(value.reshape(CHUNK // 8, 8, LANES), axis=0)
            lanes = slice(tile * LANES, (tile + 1) * LANES)
            if pi == 0:
                g_acc[:, lanes] = value
            else:
                g_acc[:, lanes] += value
            x = x + penalty[tile : tile + 1, :]
            found = x if found is None else jnp.maximum(found, x)
        if ci == 0:
            b_acc[ps, :] = found
        else:
            b_acc[ps, :] = jnp.maximum(b_acc[ps, :], found)

    here_p, here_c = [], []
    for kind, i in order:
        loads[kind, i].wait()
        if kind == "p":
            here_p.append(i)
            for ci in here_c:
                block(i, ci)
        else:
            here_c.append(i)
            for pi in here_p:
                block(pi, i)

    for t in range(tiles_c):
        part[t : t + 1, :] = jnp.sum(g_acc[:, t * LANES : (t + 1) * LANES], axis=0, keepdims=True)

    pl.semaphore_wait(barrier, n_pts - 1 + n_cand - 1)

    def exchange(axis, n, mine, src, slots, send, recv):
        for k in range(1, n):
            pltpu.make_async_remote_copy(
                src_ref=src, dst_ref=slots.at[mine], send_sem=send.at[k], recv_sem=recv.at[mine],
                device_id={axis: lax.rem(mine + k, n)}, device_id_type=MESH,
            ).start()

    def arrive(axis, n, mine, src, slots, send, recv):
        for k in range(1, n):
            other = lax.rem(mine + k, n)
            pltpu.make_async_remote_copy(
                src_ref=src, dst_ref=slots.at[other], send_sem=send.at[k], recv_sem=recv.at[other],
                device_id={axis: other}, device_id_type=MESH,
            ).wait()

    exchange("pts", n_pts, me, part, parts, part_send, part_recv)
    parts[me] = part[...]

    for t in range(tiles_p):
        turned = jnp.transpose(b_acc[t * LANES : (t + 1) * LANES, :])
        best[t : t + 1, :] = jnp.max(turned, axis=0, keepdims=True)
    exchange("cand", n_cand, mz, best, bests, best_send, best_recv)

    arrive("pts", n_pts, me, part, parts, part_send, part_recv)
    gains = parts[0]
    for k in range(1, n_pts):
        gains = gains + parts[k]
    gains_buf[...] = gains
    gains_copy = pltpu.make_async_copy(gains_buf, gains_out, out_sem.at[0])
    gains_copy.start()

    for t in range(tiles_c):
        g_col[t * LANES : (t + 1) * LANES, :] = column_tile(gains[t : t + 1, :])
    sorted_col = ranked([g_col], [gains[t : t + 1, :] for t in range(tiles_c)], TOPK)
    top_row = as_row(sorted_col)
    top[...] = top_row
    exchange("cand", n_cand, mz, top, tops, top_send, top_recv)
    tops[mz] = top_row

    arrive("cand", n_cand, mz, best, bests, best_send, best_recv)
    cover = best[...]
    for k in range(1, n_cand):
        cover = jnp.maximum(cover, bests[lax.rem(mz + k, n_cand)])
    cover_buf[...] = jnp.maximum(v_buf[...], cover * scale)
    cover_copy = pltpu.make_async_copy(cover_buf, cover_out, out_sem.at[1])
    cover_copy.start()

    arrive("cand", n_cand, mz, top, tops, top_send, top_recv)
    lists = [tops[k] for k in range(n_cand)]
    merged = ranked([column_tile(row)[:TOPK, :] for row in lists], lists, TOPK)
    top_buf[...] = as_row(merged)[:, :TOPK]
    top_copy = pltpu.make_async_copy(top_buf, top_out, out_sem.at[2])
    top_copy.start()
    gains_copy.wait()
    cover_copy.wait()
    top_copy.wait()


def solution(mesh):
    n_pts, n_cand = mesh.shape["pts"], mesh.shape["cand"]

    def on_device(points, weights, coverage, candidates, picks):
        rows, depth = points.shape
        cands = candidates.shape[0]
        tp, tc = rows // LANES, cands // LANES
        anywhere = pl.BlockSpec(memory_space=pl.ANY)
        dma = pltpu.SemaphoreType.DMA
        vmem = pltpu.VMEM
        gains, top, cover = pl.pallas_call(
            functools.partial(kernel, n_pts, n_cand),
            out_shape=(
                jax.ShapeDtypeStruct((tc, LANES), F32),
                jax.ShapeDtypeStruct((1, TOPK), F32),
                jax.ShapeDtypeStruct((tp, LANES), F32),
            ),
            in_specs=[anywhere] * 5,
            out_specs=(anywhere,) * 3,
            scratch_shapes=[
                vmem((rows, depth), points.dtype), vmem((cands, depth), candidates.dtype),
                vmem((tp, LANES), F32), vmem((tp, LANES), F32),
                pltpu.SMEM(picks.shape, jnp.int32),
                vmem((rows, LANES), F32), vmem((rows, LANES), F32),
                vmem((8, cands), F32), vmem((rows, LANES), F32),
                vmem((tc, LANES), F32), vmem((n_pts, tc, LANES), F32),
                vmem((tp, LANES), F32), vmem((n_cand, tp, LANES), F32),
                vmem((1, LANES), F32), vmem((n_cand, 1, LANES), F32),
                vmem((cands, LANES), F32),
                vmem((tc, LANES), F32), vmem((1, TOPK), F32), vmem((tp, LANES), F32),
                dma((rows // CHUNK + cands // CHUNK,)), dma((3,)), dma((3,)),
                dma((n_pts,)), dma((n_pts,)),
                dma((n_cand,)), dma((n_cand,)),
                dma((n_cand,)), dma((n_cand,)),
            ],
            compiler_params=pltpu.CompilerParams(
                collective_id=0, has_side_effects=True, vmem_limit_bytes=60 * 2**20
            ),
            name="facility",
        )(points, weights.reshape(tp, LANES), coverage.reshape(tp, LANES), candidates, picks)
        return gains.reshape(cands), top.reshape(TOPK), cover.reshape(rows)

    placed = (P("pts", None), P("pts"), P("pts"), P("cand", None), P())
    return jax.shard_map(
        on_device, mesh=mesh, in_specs=placed, out_specs=(P("cand"), P(), P("pts")), check_vma=False
    )
```

time: 56.7 us -> 23.5 us (0.41)
  blocking collectives: 35.4 us -> 0 us
  Pallas kernels: 0 us -> 18.9 us
  other arithmetic: 13.9 us -> 0 us
  matrix products: 4.37 us -> 0 us
  local copies, waits for them, and re-layouts: 1.48 us -> 3.7 us
  between operations: 1.34 us -> 0.64 us
    pallas_call x0 -> x1, Pallas kernels: none -> 18.9 us  [on_device(): pl.pallas_call(functools.partial(kernel, n_pts, n_cand), out_shape=(jax.S...]
    psum x1 -> x0, blocking collectives: 15.2 us -> none  [on_device(): gains = lax.psum(partial_value, 'pts')]
    top_k x4 -> x0, other arithmetic: 12.1 us -> none  [the longest x3 7.7 us: best_values(): return lax.top_k(jnp.concatenate([first, second]), TOPK)[0]]
    unnamed x1 -> x0, blocking collectives: 11.9 us -> none
    pmax x1 -> x0, blocking collectives: 8.34 us -> none  [on_device(): best_sim = lax.pmax(local_best, 'cand')]
    dot_general x1 -> x0, matrix products: 4.37 us -> none  [on_device(): jnp.dot(points, candidates.T, preferred_element_type=jnp.float32) * scale]
    unnamed x13 -> x3, local copies, waits for them, and re-layouts: 1.37 us -> 3.7 us
    reduce_or x1 -> x0, other arithmetic: 0.92 us -> none  [on_device(): chosen = jnp.any(picks[:, None] == columns[None, :], axis=0)]
where the time goes in v1:
time: 23.5 us; the launch traced here: 23.3 us
  Pallas kernels  18.9 us (80%)
  local copies, waits for them, and re-layouts  3.7 us (16%)
  between operations  0.64 us (3%)
    pallas_call x1, Pallas kernels, on_device(): pl.pallas_call(functools.partial(kernel, n_pts, n_cand), out_shape=(jax.S...  18.9 us
    unnamed x3, local copies, waits for them, and re-layouts  3.7 us

profile of v1, /device:TPU:0, one launch (start us, length us, event | category | flops | bytes accessed | tf_op | source)
XLA Modules:
  0.0 23.3 jit_solution(12812741257191632362)
XLA Ops:
  0.6 18.9 %facility.1 = (f32[8,128]{1,0:T(8,128)}, f32[1,64]{1,0:T(1,128)}, f32[8,128]{1,0:T(8,128)}) custom-call(bf16[1024,1024]{1,0:T(8,128)(2,1)} %points.1, f32[8,128]{1,0:T(8,128)} %bitcast.7, f32[8,128]{1,0:T(8,128)} %bitcast.8, bf16[1024,1024]{1,0:T(8,128)(2,1)} %candidates.1, s32[64]{0:T(128)} %picks.1), custom_call_target="tpu_custom_call" | custom-call | tf_op jit(solution)/shard_map/facility/pallas_call | solution.py:213
  19.6 1.3 %copy.11 = f32[1024]{0:T(1024)} copy(f32[1024]{0:T(1024)} %bitcast.6) | data formatting | bytes 8192
  20.8 1.2 %copy.12 = f32[64]{0:T(128)} copy(f32[64]{0:T(128)} %bitcast.9) | data formatting | bytes 512
  22.0 1.3 %copy.13 = f32[1024]{0:T(1024)} copy(f32[1024]{0:T(1024)} %bitcast.5) | data formatting | bytes 8192

commit v2 on v1

--- a/solution.py
+++ b/solution.py
@@ -44,10 +44,9 @@
 
 
 def kernel(
-    n_pts, n_cand, points, weights, coverage, candidates, picks, gains_out, top_out, cover_out,
+    n_pts, n_cand, points, weights, coverage, candidates, picks, gains_out, lists_out, cover_out,
     p_buf, c_buf, w_buf, v_buf, k_buf, w_col, v_col, g_acc, b_acc, part, parts, best, bests,
-    top, tops, g_col, gains_buf, top_buf, cover_buf,
-    in_sem, small_sem, out_sem, part_send, part_recv, best_send, best_recv, top_send, top_recv,
+    top, tops, g_col, in_sem, small_sem, part_send, part_recv, best_send, best_recv, top_send, top_recv,
 ):
     rows, depth = points.shape
     cands = candidates.shape[0]
@@ -169,9 +168,7 @@
     gains = parts[0]
     for k in range(1, n_pts):
         gains = gains + parts[k]
-    gains_buf[...] = gains
-    gains_copy = pltpu.make_async_copy(gains_buf, gains_out, out_sem.at[0])
-    gains_copy.start()
+    gains_out[...] = gains
 
     for t in range(tiles_c):
         g_col[t * LANES : (t + 1) * LANES, :] = column_tile(gains[t : t + 1, :])
@@ -185,15 +182,22 @@
     cover = best[...]
     for k in range(1, n_cand):
         cover = jnp.maximum(cover, bests[lax.rem(mz + k, n_cand)])
-    cover_buf[...] = jnp.maximum(v_buf[...], cover * scale)
-    cover_copy = pltpu.make_async_copy(cover_buf, cover_out, out_sem.at[1])
+    cover_out[...] = jnp.maximum(v_buf[...], cover * scale)
+
+    arrive("cand", n_cand, mz, top, tops, top_send, top_recv)
+    for k in range(n_cand):
+        lists_out[k : k + 1, :] = tops[k]
+
+
+def finish(gains, lists, cover, gains_out, top_out, cover_out, sems, top_buf):
+    gains_copy = pltpu.make_async_copy(gains, gains_out, sems.at[0])
+    cover_copy = pltpu.make_async_copy(cover, cover_out, sems.at[1])
+    gains_copy.start()
     cover_copy.start()
-
-    arrive("cand", n_cand, mz, top, tops, top_send, top_recv)
-    lists = [tops[k] for k in range(n_cand)]
-    merged = ranked([column_tile(row)[:TOPK, :] for row in lists], lists, TOPK)
+    rows = [lists[k : k + 1, :] for k in range(lists.shape[0])]
+    merged = ranked([column_tile(row)[:TOPK, :] for row in rows], rows, TOPK)
     top_buf[...] = as_row(merged)[:, :TOPK]
-    top_copy = pltpu.make_async_copy(top_buf, top_out, out_sem.at[2])
+    top_copy = pltpu.make_async_copy(top_buf, top_out, sems.at[2])
     top_copy.start()
     gains_copy.wait()
     cover_copy.wait()
@@ -210,15 +214,15 @@
         anywhere = pl.BlockSpec(memory_space=pl.ANY)
         dma = pltpu.SemaphoreType.DMA
         vmem = pltpu.VMEM
-        gains, top, cover = pl.pallas_call(
+        gains, lists, cover = pl.pallas_call(
             functools.partial(kernel, n_pts, n_cand),
             out_shape=(
-                jax.ShapeDtypeStruct((tc, LANES), F32),
-                jax.ShapeDtypeStruct((1, TOPK), F32),
-                jax.ShapeDtypeStruct((tp, LANES), F32),
+                vmem((tc, LANES), F32),
+                vmem((n_cand, LANES), F32),
+                vmem((tp, LANES), F32),
             ),
             in_specs=[anywhere] * 5,
-            out_specs=(anywhere,) * 3,
+            out_specs=(pl.BlockSpec(memory_space=vmem),) * 3,
             scratch_shapes=[
                 vmem((rows, depth), points.dtype), vmem((cands, depth), candidates.dtype),
                 vmem((tp, LANES), F32), vmem((tp, LANES), F32),
@@ -229,8 +233,7 @@
                 vmem((tp, LANES), F32), vmem((n_cand, tp, LANES), F32),
                 vmem((1, LANES), F32), vmem((n_cand, 1, LANES), F32),
                 vmem((cands, LANES), F32),
-                vmem((tc, LANES), F32), vmem((1, TOPK), F32), vmem((tp, LANES), F32),
-                dma((rows // CHUNK + cands // CHUNK,)), dma((3,)), dma((3,)),
+                dma((rows // CHUNK + cands // CHUNK,)), dma((3,)),
                 dma((n_pts,)), dma((n_pts,)),
                 dma((n_cand,)), dma((n_cand,)),
                 dma((n_cand,)), dma((n_cand,)),
@@ -240,6 +243,18 @@
             ),
             name="facility",
         )(points, weights.reshape(tp, LANES), coverage.reshape(tp, LANES), candidates, picks)
+        gains, top, cover = pl.pallas_call(
+            finish,
+            out_shape=(
+                jax.ShapeDtypeStruct((tc, LANES), F32),
+                jax.ShapeDtypeStruct((1, TOPK), F32),
+                jax.ShapeDtypeStruct((tp, LANES), F32),
+            ),
+            in_specs=[pl.BlockSpec(memory_space=vmem)] * 3,
+            out_specs=(anywhere,) * 3,
+            scratch_shapes=[dma((3,)), vmem((1, TOPK), F32)],
+            name="finish",
+        )(*(pltpu.with_memory_space_constraint(x, vmem) for x in (gains, lists, cover)))
         return gains.reshape(cands), top.reshape(TOPK), cover.reshape(rows)
 
     placed = (P("pts", None), P("pts"), P("pts"), P("cand", None), P())

time: 23.5 us -> 19.7 us (0.84)
  local copies, waits for them, and re-layouts: 3.7 us -> 0 us
    unnamed x3 -> x0, local copies, waits for them, and re-layouts: 3.7 us -> none
    pallas_call x1 -> x2, Pallas kernels: 18.9 us -> 18.9 us  [the longest x1 18.1 us: on_device(): pl.pallas_call(functools.partial(kernel, n_pts, n_cand), out_shape=(vmem(...]
where the time goes in v2:
time: 19.7 us; the launch traced here: 19.5 us
  Pallas kernels  18.9 us (96%)
  between operations  0.64 us (3%)
    pallas_call x1, Pallas kernels, on_device(): pl.pallas_call(functools.partial(kernel, n_pts, n_cand), out_shape=(vmem(...  18.1 us
    pallas_call x1, Pallas kernels, on_device(): pl.pallas_call(finish, out_shape=(jax.ShapeDtypeStruct((tc, LANES), F32),...  0.82 us

profile of v2, /device:TPU:0, one launch (start us, length us, event | category | flops | bytes accessed | tf_op | source)
XLA Modules:
  0.0 19.5 jit_solution(8134263067018710679)
XLA Ops:
  0.6 18.1 %facility.1 = (f32[8,128]{1,0:T(8,128)S(1)}, f32[4,128]{1,0:T(4,128)S(1)}, f32[8,128]{1,0:T(8,128)S(1)}) custom-call(bf16[1024,1024]{1,0:T(8,128)(2,1)} %points.1, f32[8,128]{1,0:T(8,128)} %bitcast.5, f32[8,128]{1,0:T(8,128)} %bitcast.6, bf16[1024,1024]{1,0:T(8,128)(2,1)} %candidates.1, s32[64]{0:T(128)} %picks.1), custom_call_target="tpu_custom_call" | custom-call | tf_op jit(solution)/shard_map/facility/pallas_call | solution.py:217
  18.7 0.8 %finish.1 = (f32[8,128]{1,0:T(8,128)}, f32[1,64]{1,0:T(1,128)}, f32[8,128]{1,0:T(8,128)}) custom-call(f32[8,128]{1,0:T(8,128)S(1)} %get-tuple-element.9.gains, f32[4,128]{1,0:T(4,128)S(1)} %get-tuple-element.10.lists, f32[8,128]{1,0:T(8,128)S(1)} %get-tuple-element.11.cover), custom_call_target="tpu_custom_call" | custom-call | tf_op jit(solution)/shard_map/finish/pallas_call | solution.py:246

commit v3 on v2

--- a/solution.py
+++ b/solution.py
@@ -62,6 +62,12 @@
     ]
     for copy in small:
         copy.start()
+    barrier = pltpu.get_barrier_semaphore()
+    for k in range(1, n_cand):
+        pl.semaphore_signal(
+            barrier, inc=1, device_id={"cand": lax.rem(mz + k, n_cand)}, device_id_type=MESH
+        )
+
     loads = {}
     order = []
     for i in range(max(n_p, n_c)):
@@ -75,14 +81,9 @@
         loads[kind, i] = pltpu.make_async_copy(src.at[span, :], dst.at[span, :], in_sem.at[at])
         loads[kind, i].start()
 
-    barrier = pltpu.get_barrier_semaphore()
     for k in range(1, n_pts):
         pl.semaphore_signal(
             barrier, inc=1, device_id={"pts": lax.rem(me + k, n_pts)}, device_id_type=MESH
-        )
-    for k in range(1, n_cand):
-        pl.semaphore_signal(
-            barrier, inc=1, device_id={"cand": lax.rem(mz + k, n_cand)}, device_id_type=MESH
         )
 
     for copy in small:
@@ -99,42 +100,41 @@
         w_col[t * LANES : (t + 1) * LANES, :] = column_tile(w_row[t : t + 1, :])
         v_col[t * LANES : (t + 1) * LANES, :] = column_tile(v_row[t : t + 1, :])
 
-    def block(pi, ci):
-        ps = pl.ds(pi * CHUNK, CHUNK)
+    def block(p_from, p_to, c_from, c_to):
+        ps, many = pl.ds(p_from, p_to - p_from), p_to - p_from
         sims = lax.dot_general(
-            p_buf[ps, :], c_buf[pl.ds(ci * CHUNK, CHUNK), :],
+            p_buf[ps, :], c_buf[pl.ds(c_from, c_to - c_from), :],
             (((1,), (1,)), ((), ())), preferred_element_type=F32,
         )
         w, v = w_col[ps, :], v_col[ps, :]
         found = None
-        for l in range(CHUNK // LANES):
-            tile = ci * (CHUNK // LANES) + l
-            x = sims[:, l * LANES : (l + 1) * LANES]
+        for tile in range(c_from // LANES, c_to // LANES):
+            lanes = slice(tile * LANES, (tile + 1) * LANES)
+            x = sims[:, tile * LANES - c_from : (tile + 1) * LANES - c_from]
             value = jnp.maximum(x - v, 0.0) * w
-            value = jnp.sum(value.reshape(CHUNK // 8, 8, LANES), axis=0)
-            lanes = slice(tile * LANES, (tile + 1) * LANES)
-            if pi == 0:
+            value = jnp.sum(value.reshape(many // 8, 8, LANES), axis=0)
+            if p_from == 0:
                 g_acc[:, lanes] = value
             else:
                 g_acc[:, lanes] += value
             x = x + penalty[tile : tile + 1, :]
             found = x if found is None else jnp.maximum(found, x)
-        if ci == 0:
+        if c_from == 0:
             b_acc[ps, :] = found
         else:
             b_acc[ps, :] = jnp.maximum(b_acc[ps, :], found)
 
-    here_p, here_c = [], []
+    here_p = here_c = 0
     for kind, i in order:
         loads[kind, i].wait()
         if kind == "p":
-            here_p.append(i)
-            for ci in here_c:
-                block(i, ci)
+            here_p += CHUNK
+            if here_c:
+                block(here_p - CHUNK, here_p, 0, here_c)
         else:
-            here_c.append(i)
-            for pi in here_p:
-                block(pi, i)
+            here_c += CHUNK
+            if here_p:
+                block(0, here_p, here_c - CHUNK, here_c)
 
     for t in range(tiles_c):
         part[t : t + 1, :] = jnp.sum(g_acc[:, t * LANES : (t + 1) * LANES], axis=0, keepdims=True)

time: 19.7 us -> 19.5 us (0.990)
  Pallas kernels: 18.9 us -> 18.7 us
where the time goes in v3:
time: 19.5 us; the launch traced here: 19.3 us
  Pallas kernels  18.7 us (96%)
  between operations  0.64 us (3%)
    pallas_call x1, Pallas kernels, on_device(): pl.pallas_call(functools.partial(kernel, n_pts, n_cand), out_shape=(vmem(...  17.9 us
    pallas_call x1, Pallas kernels, on_device(): pl.pallas_call(finish, out_shape=(jax.ShapeDtypeStruct((tc, LANES), F32),...  0.82 us

profile of v3, /device:TPU:0, one launch (start us, length us, event | category | flops | bytes accessed | tf_op | source)
XLA Modules:
  0.0 19.3 jit_solution(5165944395171483046)
XLA Ops:
  0.6 17.9 %facility.1 = (f32[8,128]{1,0:T(8,128)S(1)}, f32[4,128]{1,0:T(4,128)S(1)}, f32[8,128]{1,0:T(8,128)S(1)}) custom-call(bf16[1024,1024]{1,0:T(8,128)(2,1)} %points.1, f32[8,128]{1,0:T(8,128)} %bitcast.5, f32[8,128]{1,0:T(8,128)} %bitcast.6, bf16[1024,1024]{1,0:T(8,128)(2,1)} %candidates.1, s32[64]{0:T(128)} %picks.1), custom_call_target="tpu_custom_call" | custom-call | tf_op jit(solution)/shard_map/facility/pallas_call | solution.py:217
  18.5 0.8 %finish.1 = (f32[8,128]{1,0:T(8,128)}, f32[1,64]{1,0:T(1,128)}, f32[8,128]{1,0:T(8,128)}) custom-call(f32[8,128]{1,0:T(8,128)S(1)} %get-tuple-element.9.gains, f32[4,128]{1,0:T(4,128)S(1)} %get-tuple-element.10.lists, f32[8,128]{1,0:T(8,128)S(1)} %get-tuple-element.11.cover), custom_call_target="tpu_custom_call" | custom-call | tf_op jit(solution)/shard_map/finish/pallas_call | solution.py:246

commit v4 on v3

--- a/solution.py
+++ b/solution.py
@@ -64,8 +64,10 @@
         copy.start()
     barrier = pltpu.get_barrier_semaphore()
     for k in range(1, n_cand):
+        other = lax.rem(mz + k, n_cand)
+        pl.semaphore_signal(barrier, inc=1, device_id={"cand": other}, device_id_type=MESH)
         pl.semaphore_signal(
-            barrier, inc=1, device_id={"cand": lax.rem(mz + k, n_cand)}, device_id_type=MESH
+            barrier, inc=1, device_id={"pts": n_pts - 1, "cand": other}, device_id_type=MESH
         )
 
     loads = {}
@@ -139,7 +141,9 @@
     for t in range(tiles_c):
         part[t : t + 1, :] = jnp.sum(g_acc[:, t * LANES : (t + 1) * LANES], axis=0, keepdims=True)
 
-    pl.semaphore_wait(barrier, n_pts - 1 + n_cand - 1)
+    speaks = me == n_pts - 1
+    greetings = n_pts - 1 + n_cand - 1
+    pl.semaphore_wait(barrier, jnp.where(speaks, greetings + n_pts * (n_cand - 1), greetings))
 
     def exchange(axis, n, mine, src, slots, send, recv):
         for k in range(1, n):
@@ -175,7 +179,19 @@
     sorted_col = ranked([g_col], [gains[t : t + 1, :] for t in range(tiles_c)], TOPK)
     top_row = as_row(sorted_col)
     top[...] = top_row
-    exchange("cand", n_cand, mz, top, tops, top_send, top_recv)
+
+    def announce(k, p):
+        return pltpu.make_async_remote_copy(
+            src_ref=top, dst_ref=tops.at[mz], send_sem=top_send.at[k - 1, p], recv_sem=top_recv.at[mz],
+            device_id={"pts": p, "cand": lax.rem(mz + k, n_cand)}, device_id_type=MESH,
+        )
+
+    @pl.when(speaks)
+    def _():
+        for p in range(n_pts):
+            for k in range(1, n_cand):
+                announce(k, p).start()
+
     tops[mz] = top_row
 
     arrive("cand", n_cand, mz, best, bests, best_send, best_recv)
@@ -184,9 +200,20 @@
         cover = jnp.maximum(cover, bests[lax.rem(mz + k, n_cand)])
     cover_out[...] = jnp.maximum(v_buf[...], cover * scale)
 
-    arrive("cand", n_cand, mz, top, tops, top_send, top_recv)
+    for k in range(1, n_cand):
+        other = lax.rem(mz + k, n_cand)
+        pltpu.make_async_remote_copy(
+            src_ref=top, dst_ref=tops.at[other], send_sem=top_send.at[0, 0], recv_sem=top_recv.at[other],
+            device_id={"pts": n_pts - 1, "cand": other}, device_id_type=MESH,
+        ).wait_recv()
     for k in range(n_cand):
         lists_out[k : k + 1, :] = tops[k]
+
+    @pl.when(speaks)
+    def _():
+        for p in range(n_pts):
+            for k in range(1, n_cand):
+                announce(k, p).wait_send()
 
 
 def finish(gains, lists, cover, gains_out, top_out, cover_out, sems, top_buf):
@@ -236,7 +263,7 @@
                 dma((rows // CHUNK + cands // CHUNK,)), dma((3,)),
                 dma((n_pts,)), dma((n_pts,)),
                 dma((n_cand,)), dma((n_cand,)),
-                dma((n_cand,)), dma((n_cand,)),
+                dma((n_cand - 1, n_pts)), dma((n_cand,)),
             ],
             compiler_params=pltpu.CompilerParams(
                 collective_id=0, has_side_effects=True, vmem_limit_bytes=60 * 2**20

time: 19.5 us -> 19.2 us (0.985)
  Pallas kernels: 18.7 us -> 18.4 us
    pallas_call x1, Pallas kernels: 17.9 us -> 17.5 us  [on_device(): pl.pallas_call(functools.partial(kernel, n_pts, n_cand), out_shape=(vmem(...]
where the time goes in v4:
time: 19.2 us; the launch traced here: 19 us
  Pallas kernels  18.4 us (96%)
  between operations  0.64 us (3%)
    pallas_call x1, Pallas kernels, on_device(): pl.pallas_call(functools.partial(kernel, n_pts, n_cand), out_shape=(vmem(...  17.5 us
    pallas_call x1, Pallas kernels, on_device(): pl.pallas_call(finish, out_shape=(jax.ShapeDtypeStruct((tc, LANES), F32),...  0.82 us

profile of v4, /device:TPU:0, one launch (start us, length us, event | category | flops | bytes accessed | tf_op | source)
XLA Modules:
  0.0 19.0 jit_solution(15224558577083294585)
XLA Ops:
  0.6 17.5 %facility.1 = (f32[8,128]{1,0:T(8,128)S(1)}, f32[4,128]{1,0:T(4,128)S(1)}, f32[8,128]{1,0:T(8,128)S(1)}) custom-call(bf16[1024,1024]{1,0:T(8,128)(2,1)} %points.1, f32[8,128]{1,0:T(8,128)} %bitcast.5, f32[8,128]{1,0:T(8,128)} %bitcast.6, bf16[1024,1024]{1,0:T(8,128)(2,1)} %candidates.1, s32[64]{0:T(128)} %picks.1), custom_call_target="tpu_custom_call" | custom-call | tf_op jit(solution)/shard_map/facility/pallas_call | solution.py:244
  18.2 0.8 %finish.1 = (f32[8,128]{1,0:T(8,128)}, f32[1,64]{1,0:T(1,128)}, f32[8,128]{1,0:T(8,128)}) custom-call(f32[8,128]{1,0:T(8,128)S(1)} %get-tuple-element.9.gains, f32[4,128]{1,0:T(4,128)S(1)} %get-tuple-element.10.lists, f32[8,128]{1,0:T(8,128)S(1)} %get-tuple-element.11.cover), custom_call_target="tpu_custom_call" | custom-call | tf_op jit(solution)/shard_map/finish/pallas_call | solution.py:273

commit v5 on v4

--- a/solution.py
+++ b/solution.py
@@ -47,6 +47,7 @@
     n_pts, n_cand, points, weights, coverage, candidates, picks, gains_out, lists_out, cover_out,
     p_buf, c_buf, w_buf, v_buf, k_buf, w_col, v_col, g_acc, b_acc, part, parts, best, bests,
     top, tops, g_col, in_sem, small_sem, part_send, part_recv, best_send, best_recv, top_send, top_recv,
+    spoken,
 ):
     rows, depth = points.shape
     cands = candidates.shape[0]
@@ -148,27 +149,26 @@
     def exchange(axis, n, mine, src, slots, send, recv):
         for k in range(1, n):
             pltpu.make_async_remote_copy(
-                src_ref=src, dst_ref=slots.at[mine], send_sem=send.at[k], recv_sem=recv.at[mine],
+                src_ref=src, dst_ref=slots.at[mine], send_sem=send.at[0], recv_sem=recv.at[0],
                 device_id={axis: lax.rem(mine + k, n)}, device_id_type=MESH,
             ).start()
 
-    def arrive(axis, n, mine, src, slots, send, recv):
-        for k in range(1, n):
-            other = lax.rem(mine + k, n)
-            pltpu.make_async_remote_copy(
-                src_ref=src, dst_ref=slots.at[other], send_sem=send.at[k], recv_sem=recv.at[other],
-                device_id={axis: other}, device_id_type=MESH,
-            ).wait()
+    def settle(slots, n, sem):
+        view = slots.at[pl.ds(0, n)]
+        pltpu.make_async_copy(view, view, sem.at[0]).wait()
 
     exchange("pts", n_pts, me, part, parts, part_send, part_recv)
     parts[me] = part[...]
 
-    for t in range(tiles_p):
-        turned = jnp.transpose(b_acc[t * LANES : (t + 1) * LANES, :])
-        best[t : t + 1, :] = jnp.max(turned, axis=0, keepdims=True)
-    exchange("cand", n_cand, mz, best, bests, best_send, best_recv)
-
-    arrive("pts", n_pts, me, part, parts, part_send, part_recv)
+    def cover_exchange():
+        for t in range(tiles_p):
+            turned = jnp.transpose(b_acc[t * LANES : (t + 1) * LANES, :])
+            best[t : t + 1, :] = jnp.max(turned, axis=0, keepdims=True)
+        exchange("cand", n_cand, mz, best, bests, best_send, best_recv)
+
+    pl.when(jnp.logical_not(speaks))(cover_exchange)
+
+    settle(parts, n_pts - 1, part_recv)
     gains = parts[0]
     for k in range(1, n_pts):
         gains = gains + parts[k]
@@ -182,7 +182,7 @@
 
     def announce(k, p):
         return pltpu.make_async_remote_copy(
-            src_ref=top, dst_ref=tops.at[mz], send_sem=top_send.at[k - 1, p], recv_sem=top_recv.at[mz],
+            src_ref=top, dst_ref=tops.at[mz], send_sem=top_send.at[0], recv_sem=top_recv.at[0],
             device_id={"pts": p, "cand": lax.rem(mz + k, n_cand)}, device_id_type=MESH,
         )
 
@@ -191,29 +191,26 @@
         for p in range(n_pts):
             for k in range(1, n_cand):
                 announce(k, p).start()
+        cover_exchange()
 
     tops[mz] = top_row
 
-    arrive("cand", n_cand, mz, best, bests, best_send, best_recv)
+    settle(bests, n_cand - 1, best_recv)
     cover = best[...]
     for k in range(1, n_cand):
         cover = jnp.maximum(cover, bests[lax.rem(mz + k, n_cand)])
     cover_out[...] = jnp.maximum(v_buf[...], cover * scale)
 
-    for k in range(1, n_cand):
-        other = lax.rem(mz + k, n_cand)
-        pltpu.make_async_remote_copy(
-            src_ref=top, dst_ref=tops.at[other], send_sem=top_send.at[0, 0], recv_sem=top_recv.at[other],
-            device_id={"pts": n_pts - 1, "cand": other}, device_id_type=MESH,
-        ).wait_recv()
+    settle(tops, n_cand - 1, top_recv)
     for k in range(n_cand):
         lists_out[k : k + 1, :] = tops[k]
 
+    settle(parts, n_pts - 1, part_send)
+    settle(bests, n_cand - 1, best_send)
+
     @pl.when(speaks)
     def _():
-        for p in range(n_pts):
-            for k in range(1, n_cand):
-                announce(k, p).wait_send()
+        settle(spoken, n_pts * (n_cand - 1), top_send)
 
 
 def finish(gains, lists, cover, gains_out, top_out, cover_out, sems, top_buf):
@@ -261,9 +258,8 @@
                 vmem((1, LANES), F32), vmem((n_cand, 1, LANES), F32),
                 vmem((cands, LANES), F32),
                 dma((rows // CHUNK + cands // CHUNK,)), dma((3,)),
-                dma((n_pts,)), dma((n_pts,)),
-                dma((n_cand,)), dma((n_cand,)),
-                dma((n_cand - 1, n_pts)), dma((n_cand,)),
+                dma((1,)), dma((1,)), dma((1,)), dma((1,)), dma((1,)), dma((1,)),
+                vmem((n_pts * (n_cand - 1), 1, LANES), F32),
             ],
             compiler_params=pltpu.CompilerParams(
                 collective_id=0, has_side_effects=True, vmem_limit_bytes=60 * 2**20

time: 19.2 us -> 18.8 us (0.979)
  Pallas kernels: 18.4 us -> 17.9 us
    pallas_call x1, Pallas kernels: 17.5 us -> 17.1 us  [on_device(): pl.pallas_call(functools.partial(kernel, n_pts, n_cand), out_shape=(vmem(...]
where the time goes in v5:
time: 18.8 us; the launch traced here: 18.6 us
  Pallas kernels  17.9 us (95%)
  between operations  0.64 us (3%)
    pallas_call x1, Pallas kernels, on_device(): pl.pallas_call(functools.partial(kernel, n_pts, n_cand), out_shape=(vmem(...  17.1 us
    pallas_call x1, Pallas kernels, on_device(): pl.pallas_call(finish, out_shape=(jax.ShapeDtypeStruct((tc, LANES), F32),...  0.82 us

profile of v5, /device:TPU:0, one launch (start us, length us, event | category | flops | bytes accessed | tf_op | source)
XLA Modules:
  0.0 18.6 jit_solution(13321330321743983978)
XLA Ops:
  0.6 17.1 %facility.1 = (f32[8,128]{1,0:T(8,128)S(1)}, f32[4,128]{1,0:T(4,128)S(1)}, f32[8,128]{1,0:T(8,128)S(1)}) custom-call(bf16[1024,1024]{1,0:T(8,128)(2,1)} %points.1, f32[8,128]{1,0:T(8,128)} %bitcast.5, f32[8,128]{1,0:T(8,128)} %bitcast.6, bf16[1024,1024]{1,0:T(8,128)(2,1)} %candidates.1, s32[64]{0:T(128)} %picks.1), custom_call_target="tpu_custom_call" | custom-call | tf_op jit(solution)/shard_map/facility/pallas_call | solution.py:241
  17.8 0.8 %finish.1 = (f32[8,128]{1,0:T(8,128)}, f32[1,64]{1,0:T(1,128)}, f32[8,128]{1,0:T(8,128)}) custom-call(f32[8,128]{1,0:T(8,128)S(1)} %get-tuple-element.9.gains, f32[4,128]{1,0:T(4,128)S(1)} %get-tuple-element.10.lists, f32[8,128]{1,0:T(8,128)S(1)} %get-tuple-element.11.cover), custom_call_target="tpu_custom_call" | custom-call | tf_op jit(solution)/shard_map/finish/pallas_call | solution.py:269

commit v6 on v5

--- a/solution.py
+++ b/solution.py
@@ -13,7 +13,7 @@
 F32 = jnp.float32
 LOW = -1e30
 HIGH = 3e38
-CHUNK = 256
+CHUNK = 512
 
 
 def column_tile(row):

time: 18.8 us -> 17.2 us (0.915)
  Pallas kernels: 17.9 us -> 16.4 us
    pallas_call x1, Pallas kernels: 17.1 us -> 15.6 us  [on_device(): pl.pallas_call(functools.partial(kernel, n_pts, n_cand), out_shape=(vmem(...]
where the time goes in v6:
time: 17.2 us; the launch traced here: 17 us
  Pallas kernels  16.4 us (95%)
  between operations  0.64 us (4%)
    pallas_call x1, Pallas kernels, on_device(): pl.pallas_call(functools.partial(kernel, n_pts, n_cand), out_shape=(vmem(...  15.6 us
    pallas_call x1, Pallas kernels, on_device(): pl.pallas_call(finish, out_shape=(jax.ShapeDtypeStruct((tc, LANES), F32),...  0.82 us

profile of v6, /device:TPU:0, one launch (start us, length us, event | category | flops | bytes accessed | tf_op | source)
XLA Modules:
  0.0 17.0 jit_solution(8394084340165158328)
XLA Ops:
  0.6 15.6 %facility.1 = (f32[8,128]{1,0:T(8,128)S(1)}, f32[4,128]{1,0:T(4,128)S(1)}, f32[8,128]{1,0:T(8,128)S(1)}) custom-call(bf16[1024,1024]{1,0:T(8,128)(2,1)} %points.1, f32[8,128]{1,0:T(8,128)} %bitcast.5, f32[8,128]{1,0:T(8,128)} %bitcast.6, bf16[1024,1024]{1,0:T(8,128)(2,1)} %candidates.1, s32[64]{0:T(128)} %picks.1), custom_call_target="tpu_custom_call" | custom-call | tf_op jit(solution)/shard_map/facility/pallas_call | solution.py:241
  16.2 0.8 %finish.1 = (f32[8,128]{1,0:T(8,128)}, f32[1,64]{1,0:T(1,128)}, f32[8,128]{1,0:T(8,128)}) custom-call(f32[8,128]{1,0:T(8,128)S(1)} %get-tuple-element.9.gains, f32[4,128]{1,0:T(4,128)S(1)} %get-tuple-element.10.lists, f32[8,128]{1,0:T(8,128)S(1)} %get-tuple-element.11.cover), custom_call_target="tpu_custom_call" | custom-call | tf_op jit(solution)/shard_map/finish/pallas_call | solution.py:269
